TPU v7x, 32 devices: a whole 2x2x4 slice. The times are simulated.
32 devices in a mesh: seq: 8 (over y, x, core), tensor: 4 (over z).
Axes of the slice: x: 2, y: 2, z: 4, core: 2. Of those that a mesh axis runs over, the one named last changes fastest.
Arguments:
- tokens: bfloat16 [4096, 8192], P('seq', 'tensor'), may hold values from -6 to 6
- positions: int32 [4096], P('seq'), may hold values from 0 to 4095, each once
- norm_gain: float32 [8192], replicated, may hold values from 0.1 to 1.9
- w_query: bfloat16 [8192, 4096], P('seq', 'tensor'), may hold values from -0.0625 to 0.0625
- w_key: bfloat16 [8192, 1024], P('seq', 'tensor'), may hold values from -0.0625 to 0.0625
- w_value: bfloat16 [8192, 1024], P('seq', 'tensor'), may hold values from -0.0625 to 0.0625
- b_query: float32 [4096], P('tensor'), may hold values from -40 to 40
- b_key: float32 [1024], P('tensor'), may hold values from -40 to 40
- b_value: float32 [1024], P('tensor'), may hold values from -6 to 6
- w_out: bfloat16 [4096, 8192], P('tensor', 'seq'), may hold values from -0.09375 to 0.09375
Outputs:
- mixed: bfloat16 [4096, 8192], P('seq', 'tensor')
- context: bfloat16 [4096, 4096], P('seq', 'tensor')
Inputs may be any that keep to these rules, and one draw needn't show every extreme that they name: positions holds every position 0 to 4095 once.
All inputs are finite; a program needn't handle non-finite values.
Results may differ from a plain program's by a relative error of at most 0.025.
Values may be sent and summed in bfloat16 or wider, within the bound.
A program may use at most 128 MiB of HBM per device.

v0:
```python
import math

import jax
import jax.numpy as jnp
from jax import lax
from jax.sharding import PartitionSpec as P

HD = 128


NORM_EPS = 1e-06
ROPE_BASE = 1000000.0
NEG_FILL = -1e30


def rotate(values_in, positions):
    half_dim = HD // 2
    inv_freq = ROPE_BASE ** (-jnp.arange(half_dim, dtype=jnp.float32) * 2.0 / HD)
    angles = positions.astype(jnp.float32)[:, None] * inv_freq[None, :]
    cosine = jnp.cos(angles)[:, None, :]
    sines = jnp.sin(angles)[:, None, :]
    lower_half = values_in[..., :half_dim]
    upper_half = values_in[..., half_dim:]
    return jnp.concatenate(
        [lower_half * cosine - upper_half * sines, upper_half * cosine + lower_half * sines], -1
    )


def shards(tokens, positions, norm_gain, w_query, w_key, w_value, b_query, b_key, b_value, w_out):
    tok_rows = tokens.shape[0]
    features = lax.all_gather(tokens, "tensor", axis=1, tiled=True)
    inputs = features.astype(jnp.float32)
    inverse_rms = lax.rsqrt(jnp.mean(inputs * inputs, -1, keepdims=True) + NORM_EPS)
    normed = (inputs * inverse_rms * norm_gain[None, :]).astype(jnp.bfloat16)
    w_cat = jnp.concatenate((w_query, w_key, w_value), 1)
    b_cat = jnp.concatenate((b_query, b_key, b_value))
    projected = jnp.dot(
        normed, lax.all_gather(w_cat, "seq", axis=0, tiled=True), preferred_element_type=jnp.float32
    )
    projected = projected + b_cat[None, :]
    query_cols = w_query.shape[1]
    key_cols = w_key.shape[1]
    heads_here = query_cols // HD
    kv_here = key_cols // HD
    group = heads_here // kv_here
    queries = rotate(projected[:, :query_cols].reshape(tok_rows, heads_here, HD), positions).astype(
        jnp.bfloat16
    )
    queries = queries.reshape(tok_rows, kv_here, group, HD)
    keys_rot = rotate(
        projected[:, query_cols : query_cols + key_cols].reshape(tok_rows, kv_here, HD), positions
    ).astype(jnp.bfloat16)
    values = (
        projected[:, query_cols + key_cols :].astype(jnp.bfloat16).reshape(tok_rows, kv_here, HD)
    )
    scale = HD ** (-0.5)

    def attend_block(running, key_block):
        running_max, denominator, numerator = running
        block_keys, block_values, key_pos = key_block
        scores = (
            jnp.einsum("tgcd,sgd->gcts", queries, block_keys, preferred_element_type=jnp.float32)
            * scale
        )
        allowed = (key_pos[None, :] <= positions[:, None])[None, None, :, :]
        scores = jnp.where(allowed, scores, NEG_FILL)
        new_max = jnp.maximum(running_max, jnp.max(scores, -1))
        weights = jnp.where(allowed, jnp.exp(scores - new_max[..., None]), 0.0)
        rescale = jnp.exp(running_max - new_max)
        denominator = denominator * rescale + jnp.sum(weights, -1)
        numerator = numerator * rescale[..., None] + jnp.einsum(
            "gcts,sgd->gctd",
            weights.astype(jnp.bfloat16),
            block_values,
            preferred_element_type=jnp.float32,
        )
        return (new_max, denominator, numerator)

    start_state = (
        jnp.full((kv_here, group, tok_rows), NEG_FILL, jnp.float32),
        jnp.zeros((kv_here, group, tok_rows), jnp.float32),
        jnp.zeros((kv_here, group, tok_rows, HD), jnp.float32),
    )
    all_keys_in = lax.all_gather(keys_rot, "seq", axis=0, tiled=True)
    all_values_in = lax.all_gather(values, "seq", axis=0, tiled=True)
    key_pos = lax.all_gather(positions, "seq", axis=0, tiled=True)
    count = all_keys_in.shape[0]
    width = math.gcd(count, 2048)
    stacked = (
        all_keys_in.reshape(count // width, width, kv_here, HD),
        all_values_in.reshape(count // width, width, kv_here, HD),
        key_pos.reshape(count // width, width),
    )

    def stepper(carried, key_block):
        return (attend_block(carried, key_block), None)

    result, unused = lax.scan(stepper, start_state, stacked)
    unused_max, denominator, numerator = result
    per_head = numerator / denominator[..., None]
    context = (
        jnp.transpose(per_head, (2, 0, 1, 3))
        .reshape(tok_rows, heads_here * HD)
        .astype(jnp.bfloat16)
    )
    out_terms = jnp.dot(
        context,
        lax.all_gather(w_out, "seq", axis=1, tiled=True),
        preferred_element_type=jnp.float32,
    )
    summed = lax.psum_scatter(
        out_terms.astype(jnp.bfloat16), "tensor", scatter_dimension=1, tiled=True
    ).astype(jnp.float32)
    mixed = (tokens.astype(jnp.float32) + summed).astype(jnp.bfloat16)
    return (mixed, context)


def solution(mesh):
    in_specs = (
        P("seq", "tensor"),
        P("seq"),
        P(),
        P("seq", "tensor"),
        P("seq", "tensor"),
        P("seq", "tensor"),
        P("tensor"),
        P("tensor"),
        P("tensor"),
        P("tensor", "seq"),
    )
    out_specs = (P("seq", "tensor"), P("seq", "tensor"))
    return jax.shard_map(shards, mesh=mesh, in_specs=in_specs, out_specs=out_specs, check_vma=False)
```

profile of v0, /device:TPU:0, one launch (start us, length us, event | category | flops | bytes accessed | tf_op | source)
XLA Modules:
  0.0 640.7 jit_solution(5669417840117130354)
XLA Ops:
  7.2 0.0 all-gather.7.cloned.1.call-start
  7.2 0.7 all-gather.7.cloned.1.call-update
  7.9 0.0 copy-start.6
  7.9 0.0 copy-start.7
  7.9 0.0 copy-start.8
  7.9 0.0 copy-start.9
  7.9 0.0 all-gather.9.cloned.1.call-start
  8.0 3.1 pad_maximum_fusion
  11.1 0.0 all-gather.9.cloned.1.call-update
  11.2 0.0 all-gather.11.cloned.1.call-start
  11.2 0.0 copy-done.6
  11.2 0.0 copy-done.7
  11.3 0.0 copy-done.8
  11.3 0.0 copy-done.9
  11.3 1.8 multiply_cosine_fusion
  13.1 148.9 %all-gather.7.cloned.1.call-done = bf16[512,8192]{1,0:T(8,128)(2,1)} async-done(((bf16[512,2048]{1,0:T(8,128)(2,1)}), bf16[512,8192]{1,0:T(8,128)(2,1)}) %all-gather.7.cloned.1.call-update) | async-done | bytes 8388624 | tf_op jit(solution)/shard_map/all_gather | solution.py:31
  161.9 5.1 fusion.20
  167.0 120.2 %all-gather.9.cloned.1.call-done = bf16[8192,1536]{1,0:T(8,128)(2,1)} async-done(((bf16[1024,1536]{1,0:T(8,128)(2,1)}), bf16[8192,1536]{1,0:T(8,128)(2,1)}) %all-gather.9.cloned.1.call-update) | async-done | bytes 25165840 | tf_op jit(solution)/shard_map/all_gather | solution.py:38
  287.2 19.5 %fusion.27 = f32[512,1536]{1,0:T(8,128)S(1)} fusion(bf16[8192,1536]{1,0:T(8,128)(2,1)} %all-gather.9.cloned.1.call-done, bf16[512,8192]{1,0:T(8,128)(2,1)} %all-gather.7.cloned.1.call-done, f32[8192]{0:T(1024)S(1)} %copy-done.10, f32[512]{0:T(512)S(1)} %add_rsqrt_fusion, f32[1536]{0:T(1024)S(1)} %pad_maximum_fusion.3), kind=kOutput, calls=%fused_computation.35 | convolution fusion | flops 12902465536 | bytes 36741120 | tf_op jit(solution)/shard_map/dot_general | solution.py:37
  306.7 0.0 copy-start.1
  306.7 1.6 copy-done.1
  308.4 0.3 reshape.122
  308.7 0.6 fusion.32
  309.3 1.2 subtract_convert_fusion.1
  310.6 0.8 pad_maximum_fusion.2
  311.4 0.0 all-gather.11.cloned.1.call-update
  311.4 0.0 all-gather.13.cloned.1.call-start
  311.5 1.8 copy_bitcast_fusion
  313.2 0.0 all-gather.13.cloned.1.call-update
  313.3 0.0 all-gather.15.cloned.1.call-start
  313.3 0.5 all-gather.15.cloned.1.call-update
  313.9 0.0 reduce-scatter.2.cloned.1.call-start
  313.9 8.9 %all-gather = s32[8,1,512]{2,1,0:T(1,128)S(1)} all-gather(s32[1,1,512]{2,1,0:T(1,128)S(1)} %bitcast.69), channel_id=1, replica_groups=mesh['seq'=8,'tensor'=4] {'seq'}, dimensions={0}, use_global_device_ids=true | all-gather | bytes 18432 | tf_op jit(solution)/shard_map/all_gather | solution.py:86
  322.9 0.0 copy-done.2
  322.9 0.0 copy-start.3
  322.9 0.2 slice_bitcast_fusion
  323.1 0.5 copy.42
  323.5 0.3 copy-done.3
  323.8 0.8 subtract_convert_fusion
  324.7 0.0 copy-start.4
  324.7 0.1 copy.28
  324.8 0.1 copy.29
  325.0 1.5 pad_maximum_fusion.1
  326.5 12.8 %all-gather.11.cloned.1.call-done = bf16[4096,2,128]{2,0,1:T(8,128)(2,1)} async-done(((bf16[512,2,128]{2,0,1:T(8,128)(2,1)}), bf16[4096,2,128]{2,0,1:T(8,128)(2,1)}) %all-gather.11.cloned.1.call-update) | async-done | bytes 2097168 | tf_op jit(solution)/shard_map/all_gather | solution.py:84
  339.3 29.6 %all-gather.13.cloned.1.call-done = bf16[4096,2,128]{2,0,1:T(8,128)(2,1)} async-done(((bf16[512,2,128]{2,0,1:T(8,128)(2,1)}), bf16[4096,2,128]{2,0,1:T(8,128)(2,1)}) %all-gather.13.cloned.1.call-update) | async-done | bytes 2097168 | tf_op jit(solution)/shard_map/all_gather | solution.py:85
  368.9 97.0 %while.15 = (s32[]{:T(128)}, f32[2,4,512]{2,1,0:T(4,128)S(1)}, f32[2,4,512]{2,1,0:T(4,128)S(1)}, f32[2,4,512,128]{3,2,1,0:T(8,128)S(1)}, s32[2,2048]{1,0:T(2,128...) while((s32[]{:T(128)}, f32[2,4,512]{2,1,0:T(4,128)S(1)}, ...), condition=%wide.region_4.5_spmd.clone, body=%wide.region_1.4_spmd.clone.sunk | while | flops 4406661120 | bytes 112487544 | solution.py:98
  368.9 0.8 broadcast_compare_fusion.2
  369.7 16.7 %fusion.48 = (f32[2,4,512]{2,1,0:T(4,128)S(1)}, f32[2,2048,512,4]{2,1,3,0:T(8,128)}) fusion(pred[512,2048]{0,1:T(8,128)(4,1)S(1)} %broadcast_compare_fusion.2, bf16[512,2,4,128]{3,0,2,1:T(8,128)(2,1)} %get-tuple-element.222, bf16[2,2048,2,128]{3,1,0,2:T(8,128)(2,1)} %get-tuple-element.221, s32[]{:T(128)} %get-tuple-element.204), kind=kOutput, calls=%fused_computation.2.clone.1 | convolution fusion | flops 2172645376 | bytes 36717056 | tf_op jit(solution)/shard_map/while/body/eval_jaxpr/tgcd,sgd->gcts/dot_general | solution.py:62
  386.4 14.9 %fusion.49 = f32[2,4,512]{2,1,0:T(4,128)S(1)} fusion(f32[2,2048,512,4]{2,1,3,0:T(8,128)} %get-tuple-element.190, f32[2,4,512]{2,1,0:T(4,128)S(1)} %select_maximum_fusion.2, pred[512,2048]{0,1:T(8,128)(4,1)S(1)} %broadcast_compare_fusion.2), kind=kLoop, calls=%fused_computation.4.clone.1 | loop fusion | flops 41938944 | bytes 34635776 | tf_op jit(solution)/shard_map/while/body/eval_jaxpr/reduce_sum | solution.py:70
  401.3 17.8 %fusion.51 = f32[2,4,512,128]{3,2,1,0:T(8,128)S(1)} fusion(f32[2,4,512,128]{3,2,1,0:T(8,128)S(1)} %get-tuple-element.207, f32[2,2048,512,4]{2,1,3,0:T(8,128)} %get-tuple-element.190, f32[2,4,512]{2,1,0:T(4,128)S(1)} %select_maximum_fusion.2, pred[512,2048]{0,1:T(8,128)(4,1)S(1)} %broadcast_compare_fusion.2, ...), kind=kOutput, calls=%fused_computation.8.clone.1 | convolution fusion | flops 2190999552 | bytes 39879168 | tf_op jit(solution)/shard_map/while/body/eval_jaxpr/gcts,sgd->gctd/dot_general | solution.py:71
  419.2 0.8 broadcast_compare_fusion.2
  420.0 15.0 %fusion.48 = (f32[2,4,512]{2,1,0:T(4,128)S(1)}, f32[2,2048,512,4]{2,1,3,0:T(8,128)}) fusion(pred[512,2048]{0,1:T(8,128)(4,1)S(1)} %broadcast_compare_fusion.2, bf16[512,2,4,128]{3,0,2,1:T(8,128)(2,1)} %get-tuple-element.222, bf16[2,2048,2,128]{3,1,0,2:T(8,128)(2,1)} %get-tuple-element.221, s32[]{:T(128)} %get-tuple-element.204), kind=kOutput, calls=%fused_computation.2.clone.1 | convolution fusion | flops 2172645376 | bytes 36717056 | tf_op jit(solution)/shard_map/while/body/eval_jaxpr/tgcd,sgd->gcts/dot_general | solution.py:62
  435.0 15.4 %fusion.49 = f32[2,4,512]{2,1,0:T(4,128)S(1)} fusion(f32[2,2048,512,4]{2,1,3,0:T(8,128)} %get-tuple-element.190, f32[2,4,512]{2,1,0:T(4,128)S(1)} %select_maximum_fusion.2, pred[512,2048]{0,1:T(8,128)(4,1)S(1)} %broadcast_compare_fusion.2), kind=kLoop, calls=%fused_computation.4.clone.1 | loop fusion | flops 41938944 | bytes 34635776 | tf_op jit(solution)/shard_map/while/body/eval_jaxpr/reduce_sum | solution.py:70
  450.4 15.5 %fusion.51 = f32[2,4,512,128]{3,2,1,0:T(8,128)S(1)} fusion(f32[2,4,512,128]{3,2,1,0:T(8,128)S(1)} %get-tuple-element.207, f32[2,2048,512,4]{2,1,3,0:T(8,128)} %get-tuple-element.190, f32[2,4,512]{2,1,0:T(4,128)S(1)} %select_maximum_fusion.2, pred[512,2048]{0,1:T(8,128)(4,1)S(1)} %broadcast_compare_fusion.2, ...), kind=kOutput, calls=%fused_computation.8.clone.1 | convolution fusion | flops 2190999552 | bytes 39879168 | tf_op jit(solution)/shard_map/while/body/eval_jaxpr/gcts,sgd->gctd/dot_general | solution.py:71
  465.9 0.7 fusion.30
  466.6 0.8 copy.33
  467.5 0.8 convert_element_type.44
  468.2 0.0 copy-start.5
  468.2 0.0 all-gather.15.cloned.1.call-done
  468.3 17.2 %convolution_convert_fusion = bf16[512,8192]{1,0:T(8,128)(2,1)} fusion(bf16[512,1024]{1,0:T(8,128)(2,1)S(1)} %convert_element_type.44, bf16[1024,8192]{1,0:T(8,128)(2,1)} %all-gather.15.cloned.1.call-done), kind=kOutput, calls=%fused_computation.30 | convolution fusion | flops 8594128896 | bytes 26214400 | tf_op jit(solution)/shard_map/dot_general | solution.py:106
  485.4 0.0 reduce-scatter.2.cloned.1.call-update
  485.5 144.7 %reduce-scatter.2.cloned.1.call-done = bf16[512,2048]{1,0:T(8,128)(2,1)} async-done(((bf16[512,8192]{1,0:T(8,128)(2,1)}), bf16[512,2048]{1,0:T(8,128)(2,1)}) %reduce-scatter.2.cloned.1.call-update) | async-done | bytes 2097168 | tf_op jit(solution)/shard_map/reduce_scatter | solution.py:111
  630.2 0.0 copy-done
  630.2 3.7 add_convert_fusion
  (24 shorter events, 0.2 us)
Async XLA Ops:
  7.2 154.7 %all-gather.7.cloned.1.call-start = ((), (), s32[]{:S(2)}) async-start(), calls=%async_computation.1 | async-start | bytes 10485760 | tf_op jit(solution)/shard_map/all_gather | solution.py:31
  7.9 3.3 copy-start.6
  7.9 3.3 copy-start.7
  7.9 3.3 copy-start.8
  7.9 3.3 copy-start.9
  7.9 279.3 %all-gather.9.cloned.1.call-start = ((), (), s32[]{:S(2)}) async-start(), calls=%async_computation.2 | async-start | bytes 28311552 | tf_op jit(solution)/shard_map/all_gather | solution.py:38
  11.2 328.2 %all-gather.11.cloned.1.call-start = ((), (), s32[]{:S(2)}) async-start(), calls=%async_computation.3 | async-start | bytes 2359296 | tf_op jit(solution)/shard_map/all_gather | solution.py:84
  13.1 274.2 %copy-start.10 = (f32[8192]{0:T(1024)S(1)}, f32[8192]{0:T(1024)}, u32[]{:S(2)}) copy-start(f32[8192]{0:T(1024)} %param.14) | copy-start | bytes 98308
  306.7 1.7 copy-start.1
  309.3 13.6 %copy-start.2 = (f32[512,1536]{1,0:T(8,128)S(1)}, f32[512,1536]{1,0:T(8,128)}, u32[]{:S(2)}) copy-start(f32[512,1536]{1,0:T(8,128)} %copy-done.1) | copy-start | bytes 9437188
  311.4 57.5 %all-gather.13.cloned.1.call-start = ((), (), s32[]{:S(2)}) async-start(), calls=%async_computation.4 | async-start | bytes 2359296 | tf_op jit(solution)/shard_map/all_gather | solution.py:85
  313.3 155.0 %all-gather.15.cloned.1.call-start = ((), (), s32[]{:S(2)}) async-start(), calls=%async_computation.5 | async-start | bytes 18874368 | tf_op jit(solution)/shard_map/all_gather | solution.py:108
  313.9 316.3 %reduce-scatter.2.cloned.1.call-start = ((), (), s32[]{:S(2)}) async-start(), calls=%async_computation.6 | async-start | bytes 10485760 | tf_op jit(solution)/shard_map/reduce_scatter | solution.py:111
  322.9 1.0 copy-start.3
  324.7 44.3 %copy-start.4 = (f32[2,4,512,128]{3,2,1,0:T(8,128)S(1)}, f32[2,4,512,128]{3,2,1,0:T(8,128)}, u32[]{:S(2)}) copy-start(f32[2,4,512,128]{3,2,1,0:T(8,128)} %custom-call.2) | copy-start | bytes 6291460
  468.2 17.2 %copy-start.5 = (bf16[512,1024]{1,0:T(8,128)(2,1)}, bf16[512,1024]{1,0:T(8,128)(2,1)S(1)}, u32[]{:S(2)}) copy-start(bf16[512,1024]{1,0:T(8,128)(2,1)S(1)} %convert_element_type.44) | copy-start | bytes 3145732
  485.4 144.7 %copy-start = (bf16[512,2048]{1,0:T(8,128)(2,1)S(1)}, bf16[512,2048]{1,0:T(8,128)(2,1)}, u32[]{:S(2)}) copy-start(bf16[512,2048]{1,0:T(8,128)(2,1)} %param.12) | copy-start | bytes 6291460
Sparse Core Ops, SparseCore 0:
  9.5 152.3 all-gather.6
  163.8 123.3 all-gather.8
  311.5 27.7 all-gather.10
  341.1 27.7 all-gather.12
  370.7 89.7 all-gather.14
  485.6 144.5 reduce-scatter.1
where the time goes:
time: 641 us
  waiting for transfers between devices  457 us (71%)
  matrix products  102 us (16%)
  other arithmetic  50.8 us (8%)
  between operations  14.4 us (2%)
  blocking collectives  8.87 us (1%)
  local copies, waits for them, and re-layouts  7.19 us (1%)
    all_gather x1, waiting for transfers between devices, shards(): features = lax.all_gather(tokens, 'tensor', axis=1, tiled=True)  149 us
    reduce_scatter x1, waiting for transfers between devices, shards(): lax.psum_scatter(out_terms.astype(jnp.bfloat16), 'tensor', scatter_dimens...  145 us
    all_gather x1, waiting for transfers between devices, shards(): lax.all_gather(w_cat, 'seq', axis=0, tiled=True)  120 us
    dot_general x2, matrix products, attend_block(): jnp.einsum('gcts,sgd->gctd', weights.astype(jnp.bfloat16), block_values,...  33.3 us
    dot_general x2, matrix products, attend_block(): jnp.einsum('tgcd,sgd->gcts', queries, block_keys, preferred_element_type=...  31.7 us
    reduce_sum x2, other arithmetic, attend_block(): denominator = denominator * rescale + jnp.sum(weights, -1)  30.2 us
    all_gather x1, waiting for transfers between devices, shards(): all_values_in = lax.all_gather(values, 'seq', axis=0, tiled=True)  29.6 us
    dot_general x1, matrix products, shards(): jnp.dot(normed, lax.all_gather(w_cat, 'seq', axis=0, tiled=True), preferr...  19.5 us
  transfers between devices with their start and end apart: 6, of which 5 were waited for; matrix products, arithmetic and copies ran while one was open for 18% of the time, Pallas kernels for 0%

commit v1 on v0

v1 whole, which is shorter than its diff:
```python
import functools

import jax
import jax.numpy as jnp
from jax import lax
from jax.experimental import pallas as pl
from jax.experimental.pallas import tpu as pltpu
from jax.sharding import PartitionSpec as P


HD = 128


NORM_EPS = 1e-06
ROPE_BASE = 1000000.0
NEG_FILL = -1e30
CHUNKS = 4
MESH = pl.DeviceIdType.MESH
ANY = pl.BlockSpec(memory_space=pl.ANY)


def rotate(values_in, positions):
    half_dim = HD // 2
    inv_freq = ROPE_BASE ** (-jnp.arange(half_dim, dtype=jnp.float32) * 2.0 / HD)
    angles = positions.astype(jnp.float32)[:, None] * inv_freq[None, :]
    cosine = jnp.cos(angles)[:, None, :]
    sines = jnp.sin(angles)[:, None, :]
    lower_half = values_in[..., :half_dim]
    upper_half = values_in[..., half_dim:]
    return jnp.concatenate(
        [lower_half * cosine - upper_half * sines, upper_half * cosine + lower_half * sines], -1
    )


def gather_line_kernel(n, src, out, stage, send_sem, recv_sem, local_sem):
    me = lax.axis_index("tensor")
    width = src.shape[1]

    def slot(block):
        return out.at[:, pl.ds(pl.multiple_of(block * width, 128), width)]

    barrier = pltpu.get_barrier_semaphore()
    for other in ((me + 1) % n, (me + n - 1) % n):
        pl.semaphore_signal(barrier, inc=1, device_id={"tensor": other}, device_id_type=MESH)
    pl.semaphore_wait(barrier, 2)

    def copy(way, step, block, first, target):
        return pltpu.make_async_remote_copy(
            src_ref=src if first else slot(block),
            dst_ref=slot(block),
            send_sem=send_sem.at[way, step],
            recv_sem=recv_sem.at[way, step],
            device_id={"tensor": target},
            device_id_type=MESH,
        )

    def sends(step):
        right = (me >= step) & (me < n - 1)
        left = (me + step < n) & (me > 0)
        return (right, 0, me - step, me + 1), (left, 1, me + step, me - 1)

    for step in range(n - 1):
        for cond, way, block, target in sends(step):

            @pl.when(cond)
            def _():
                copy(way, step, block, step == 0, target).start()

        if step == 0:
            load = pltpu.make_async_copy(src, stage, local_sem.at[0])
            load.start()
            load.wait()
            store = pltpu.make_async_copy(stage, slot(me), local_sem.at[1])
            store.start()
            store.wait()

        @pl.when(me - 1 - step >= 0)
        def _():
            copy(0, step, me - 1 - step, False, me - 1).wait_recv()

        @pl.when(me + 1 + step < n)
        def _():
            copy(1, step, me + 1 + step, False, me + 1).wait_recv()

    for step in range(n - 1):
        for cond, way, block, target in sends(step):

            @pl.when(cond)
            def _():
                copy(way, step, block, step == 0, target).wait_send()


def gather_line(n, block):
    rows, width = block.shape
    return pl.pallas_call(
        functools.partial(gather_line_kernel, n),
        out_shape=jax.ShapeDtypeStruct((rows, n * width), block.dtype),
        in_specs=[ANY],
        out_specs=ANY,
        scratch_shapes=[
            pltpu.VMEM((rows, width), block.dtype),
            pltpu.SemaphoreType.DMA((2, n - 1)),
            pltpu.SemaphoreType.DMA((2, n - 1)),
            pltpu.SemaphoreType.DMA((2,)),
        ],
        compiler_params=pltpu.CompilerParams(collective_id=0, has_side_effects=True),
        cost_estimate=pl.CostEstimate(flops=10**11, bytes_accessed=3 * 10**8, transcendentals=0),
    )(block)


def gather_pairs_kernel(n, kv, pos, kv_out, pos_out, kv_stage, pos_stage, send_sem, recv_sem, local_sem):
    me = lax.axis_index("seq")
    twin = me + 1 - 2 * (me % 2)
    pairs = n // 2

    barrier = pltpu.get_barrier_semaphore()
    for other in [(me + 2 * j) % n for j in range(1, pairs)] + [twin]:
        pl.semaphore_signal(barrier, inc=1, device_id={"seq": other}, device_id_type=MESH)
    pl.semaphore_wait(barrier, pairs)

    arrays = ((kv, kv_out, kv_stage), (pos, pos_out, pos_stage))

    def copy(which, hop, j, block, own, target):
        source, dest, _ = arrays[which]
        return pltpu.make_async_remote_copy(
            src_ref=source if own else dest.at[block],
            dst_ref=dest.at[block],
            send_sem=send_sem.at[which, hop, j],
            recv_sem=recv_sem.at[which, hop, j],
            device_id={"seq": target},
            device_id_type=MESH,
        )

    for which in range(2):
        for j in range(1, pairs):
            copy(which, 0, j, me, True, (me + 2 * j) % n).start()
        copy(which, 1, 0, me, True, twin).start()
    for which in range(2):
        source, dest, stage = arrays[which]
        load = pltpu.make_async_copy(source, stage, local_sem.at[which, 0])
        load.start()
        load.wait()
        store = pltpu.make_async_copy(stage, dest.at[me], local_sem.at[which, 1])
        store.start()
        store.wait()
    for j in range(1, pairs):
        origin = (me + n - 2 * j) % n
        for which in range(2):
            copy(which, 0, j, origin, False, origin).wait_recv()
            copy(which, 1, j, origin, False, twin).start()
    for j in range(pairs):
        for which in range(2):
            copy(which, 1, j, (twin + n - 2 * j) % n, False, twin).wait_recv()
    for which in range(2):
        for j in range(1, pairs):
            copy(which, 0, j, me, True, (me + 2 * j) % n).wait_send()
        copy(which, 1, 0, me, True, twin).wait_send()
        for j in range(1, pairs):
            copy(which, 1, j, (me + n - 2 * j) % n, False, twin).wait_send()


def gather_pairs(n, kv, pos):
    sems = pltpu.SemaphoreType.DMA((2, 2, n // 2))
    return pl.pallas_call(
        functools.partial(gather_pairs_kernel, n),
        out_shape=(
            jax.ShapeDtypeStruct((n, *kv.shape), kv.dtype),
            jax.ShapeDtypeStruct((n, *pos.shape), pos.dtype),
        ),
        in_specs=[ANY, ANY],
        out_specs=(ANY, ANY),
        scratch_shapes=[
            pltpu.VMEM(kv.shape, kv.dtype),
            pltpu.VMEM(pos.shape, pos.dtype),
            sems,
            sems,
            pltpu.SemaphoreType.DMA((2, 2)),
        ],
        compiler_params=pltpu.CompilerParams(collective_id=1, has_side_effects=True),
        cost_estimate=pl.CostEstimate(flops=2 * 10**10, bytes_accessed=6 * 10**7, transcendentals=0),
    )(kv, pos)


def attend(queries, all_keys, all_values, key_pos, positions):
    scores = jnp.einsum("tgcd,sgd->gcts", queries, all_keys, preferred_element_type=jnp.float32)
    scores = scores * HD ** (-0.5)
    allowed = (key_pos[None, :] <= positions[:, None])[None, None, :, :]
    scores = jnp.where(allowed, scores, NEG_FILL)
    row_max = jnp.max(scores, -1, keepdims=True)
    weights = jnp.where(allowed, jnp.exp(scores - row_max), 0.0)
    denominator = jnp.sum(weights, -1)
    numerator = jnp.einsum(
        "gcts,sgd->gctd",
        weights.astype(jnp.bfloat16),
        all_values,
        preferred_element_type=jnp.float32,
    )
    per_head = numerator / denominator[..., None]
    return (
        jnp.transpose(per_head, (2, 0, 1, 3)).reshape(queries.shape[0], -1).astype(jnp.bfloat16)
    )


def reduce_terms(terms):
    return lax.psum_scatter(terms, "tensor", scatter_dimension=1, tiled=True)


def shards(seq, tensor, tokens, positions, norm_gain, w_query, w_key, w_value, b_query, b_key, b_value, w_out):
    tok_rows = tokens.shape[0]
    w_cat = jnp.concatenate((w_query, w_key, w_value), 1)
    b_cat = jnp.concatenate((b_query, b_key, b_value))
    w_all = lax.all_gather(w_cat, "seq", axis=0, tiled=True)
    features = gather_line(tensor, tokens)
    w_all, features, w_out = lax.optimization_barrier((w_all, features, w_out))
    inputs = features.astype(jnp.float32)
    inverse_rms = lax.rsqrt(jnp.mean(inputs * inputs, -1, keepdims=True) + NORM_EPS)
    normed = (inputs * inverse_rms * norm_gain[None, :]).astype(jnp.bfloat16)
    w_out_all = lax.all_gather(w_out, "seq", axis=1, tiled=True)
    projected = jnp.dot(normed, w_all, preferred_element_type=jnp.float32) + b_cat[None, :]
    query_cols = w_query.shape[1]
    key_cols = w_key.shape[1]
    heads_here = query_cols // HD
    kv_here = key_cols // HD
    group = heads_here // kv_here
    queries = rotate(projected[:, :query_cols].reshape(tok_rows, heads_here, HD), positions).astype(
        jnp.bfloat16
    )
    queries = queries.reshape(tok_rows, kv_here, group, HD)
    keys_rot = rotate(
        projected[:, query_cols : query_cols + key_cols].reshape(tok_rows, kv_here, HD), positions
    ).astype(jnp.bfloat16)
    values = projected[:, query_cols + key_cols :].astype(jnp.bfloat16)
    kv = jnp.concatenate((keys_rot.reshape(tok_rows, key_cols), values), 1)
    kv_all, pos_all = gather_pairs(seq, kv, jnp.broadcast_to(positions[None, :], (8, tok_rows)))
    all_keys = kv_all[:, :, :key_cols].reshape(seq * tok_rows, kv_here, HD)
    all_values = kv_all[:, :, key_cols:].reshape(seq * tok_rows, kv_here, HD)
    key_pos = pos_all[:, 0, :].reshape(seq * tok_rows)

    size = tok_rows // CHUNKS
    contexts, sums = [], []
    terms = None
    for chunk in range(CHUNKS):
        rows = slice(chunk * size, (chunk + 1) * size)
        part = queries[rows]
        if terms is not None:
            part, terms = lax.optimization_barrier((part, terms))
            sums.append(reduce_terms(terms))
        context = attend(part, all_keys, all_values, key_pos, positions[rows])
        contexts.append(context)
        terms = jnp.dot(context, w_out_all, preferred_element_type=jnp.float32).astype(jnp.bfloat16)
    sums.append(reduce_terms(terms))
    summed = jnp.concatenate(sums, 0).astype(jnp.float32)
    mixed = (tokens.astype(jnp.float32) + summed).astype(jnp.bfloat16)
    return (mixed, jnp.concatenate(contexts, 0))


def solution(mesh):
    in_specs = (
        P("seq", "tensor"),
        P("seq"),
        P(),
        P("seq", "tensor"),
        P("seq", "tensor"),
        P("seq", "tensor"),
        P("tensor"),
        P("tensor"),
        P("tensor"),
        P("tensor", "seq"),
    )
    out_specs = (P("seq", "tensor"), P("seq", "tensor"))

    def body(*args):
        return shards(mesh.shape["seq"], mesh.shape["tensor"], *args)

    return jax.shard_map(body, mesh=mesh, in_specs=in_specs, out_specs=out_specs, check_vma=False)
```

time: 641 us -> 540 us (0.84)
  waiting for transfers between devices: 457 us -> 179 us
  Pallas kernels: 0 us -> 176 us
  other arithmetic: 50.8 us -> 20.6 us
  matrix products: 102 us -> 124 us
  local copies, waits for them, and re-layouts: 7.19 us -> 22.3 us
  blocking collectives: 8.87 us -> 0 us
    all_gather x5 -> x2, waiting for transfers between devices: 311 us -> 1.72 us  [the longest x1 1.7 us: shards(): w_out_all = lax.all_gather(w_out, 'seq', axis=1, tiled=True)]
    pallas_call x0 -> x2, Pallas kernels: none -> 176 us  [the longest x1 143 us: gather_line(): pl.pallas_call(functools.partial(gather_line_kernel, n), out_shape=jax.Sh...]
    sub x0 -> x4, matrix products: none -> 46.2 us  [attend(): weights = jnp.where(allowed, jnp.exp(scores - row_max), 0.0)]
    reduce_scatter x1 -> x4, waiting for transfers between devices: 145 us -> 175 us  [reduce_terms(): return lax.psum_scatter(terms, 'tensor', scatter_dimension=1, tiled=True)]
    reduce_sum x2 -> x0, other arithmetic: 30.2 us -> none  [attend_block(): denominator = denominator * rescale + jnp.sum(weights, -1)]
    dot_general x6 -> x9, matrix products: 102 us -> 77.7 us  [the longest x4 38.5 us: shards(): jnp.dot(context, w_out_all, preferred_element_type=jnp.float32)]
    all_gather x1 -> x0, blocking collectives: 8.87 us -> none  [shards(): key_pos = lax.all_gather(positions, 'seq', axis=0, tiled=True)]
    slice x1 -> x8, local copies, waits for them, and re-layouts: 0.61 us -> 7.83 us  [the longest x1 3.86 us: shards(): all_keys = kv_all[:, :, :key_cols].reshape(seq * tok_rows, kv_here, HD)]
  transfers between devices with their start and end apart: 6 -> 6, of which waited for: 5 -> 5; matrix products, arithmetic and copies ran while one was open for 18% -> 13% of each run, Pallas kernels for 0% -> 33%
where the time goes in v1:
time: 540 us; the launch traced here: 537 us
  waiting for transfers between devices  179 us (33%)
  Pallas kernels  176 us (33%)
  matrix products  124 us (23%)
  local copies, waits for them, and re-layouts  22.3 us (4%)
  other arithmetic  20.6 us (4%)
  between operations  14.7 us (3%)
    reduce_scatter x4, waiting for transfers between devices, reduce_terms(): return lax.psum_scatter(terms, 'tensor', scatter_dimension=1, tiled=True)  175 us
    pallas_call x1, Pallas kernels, gather_line(): pl.pallas_call(functools.partial(gather_line_kernel, n), out_shape=jax.Sh...  143 us
    sub x4, matrix products, attend(): weights = jnp.where(allowed, jnp.exp(scores - row_max), 0.0)  46.2 us
    dot_general x4, matrix products, shards(): jnp.dot(context, w_out_all, preferred_element_type=jnp.float32)  38.5 us
    pallas_call x1, Pallas kernels, gather_pairs(): pl.pallas_call(functools.partial(gather_pairs_kernel, n), out_shape=(jax....  33.3 us
    dot_general x4, matrix products, attend(): jnp.einsum('gcts,sgd->gctd', weights.astype(jnp.bfloat16), all_values, pr...  20.5 us
    dot_general x1, matrix products, shards(): jnp.dot(normed, w_all, preferred_element_type=jnp.float32) + b_cat[None, :]  18.7 us
  transfers between devices with their start and end apart: 6, of which 5 were waited for; matrix products, arithmetic and copies ran while one was open for 13% of the time, Pallas kernels for 33%

profile of v1, /device:TPU:0, one launch (start us, length us, event | category | flops | bytes accessed | tf_op | source)
XLA Modules:
  0.0 536.7 jit_solution(7437176312294872484)
XLA Ops:
  7.2 0.0 all-gather.3.cloned.1.call-start
  7.2 3.3 pad_maximum_fusion
  10.5 0.0 all-gather.3.cloned.1.call-update
  10.5 0.0 copy-start.6
  10.5 0.0 all-gather.5.cloned.1.call-start
  10.6 143.0 %shard_map.113 = bf16[512,8192]{1,0:T(8,128)(2,1)} custom-call(bf16[512,2048]{1,0:T(8,128)(2,1)} %src.1), custom_call_target="tpu_custom_call" | custom-call | flops 99999997952 | bytes 300000000 | tf_op jit(solution)/shard_map/pallas_call | solution.py:95
  153.6 0.0 all-gather.3.cloned.1.call-done
  153.6 0.0 all-gather.5.cloned.1.call-update
  153.6 0.0 reduce-scatter.11.cloned.1.call-start
  153.8 1.0 multiply_cosine_fusion
  154.8 5.3 fusion.4
  160.0 0.6 copy-done
  160.6 18.7 %fusion.35 = f32[512,1536]{1,0:T(8,128)S(1)} fusion(bf16[8192,1536]{1,0:T(8,128)(2,1)} %all-gather.3.cloned.1.call-done, bf16[512,8192]{1,0:T(8,128)(2,1)S(1)} %copy-done, f32[8192]{0:T(1024)S(1)} %copy-done.10, f32[512]{0:T(512)S(1)} %add_rsqrt_fusion, f32[1536]{0:T(1024)S(1)} %pad_maximum_fusion.5), kind=kOutput, calls=%fused_computation.49 | convolution fusion | flops 12902465536 | bytes 36741120 | tf_op jit(solution)/shard_map/dot_general | solution.py:219
  179.4 1.6 copy-done.1
  181.1 0.3 reshape.220
  181.4 0.8 subtract_convert_fusion.1
  182.2 0.7 pad_maximum_fusion.4
  182.9 0.8 pad_maximum_fusion.2.kv
  183.8 0.6 broadcast_in_dim.81.pos
  184.4 33.3 %shard_map.114 = (bf16[8,512,512]{2,1,0:T(8,128)(2,1)}, s32[8,8,512]{2,1,0:T(8,128)}) custom-call(bf16[512,512]{1,0:T(8,128)(2,1)} %pad_maximum_fusion.2.kv, s32[8,512]{1,0:T(8,128)} %broadcast_in_dim.81.pos), custom_call_target="tpu_custom_call" | custom-call | flops 20000000000 | bytes 60000000 | tf_op jit(solution)/shard_map/pallas_call | solution.py:164
  217.7 0.9 slice.76
  218.6 3.9 fusion.121
  222.5 2.0 reshape.221
  224.5 1.7 slice_bitcast_fusion
  226.3 0.5 copy.60
  226.7 0.9 subtract_convert_fusion
  227.6 0.6 fusion.112
  228.2 0.7 copy.13
  228.9 2.6 reshape.222
  231.5 3.8 copy.34
  235.3 0.7 copy.12
  236.1 0.8 copy.17
  236.8 0.8 copy.21
  237.6 2.5 broadcast_compare_fusion.3
  240.1 12.8 %fusion.123 = (f32[2,4,128]{2,1,0:T(4,128)S(1)}, bf16[2,4,128,4096]{2,3,1,0:T(8,128)(2,1)}) fusion(pred[128,4096]{0,1:T(8,128)(4,1)} %get-tuple-element.34, bf16[128,2,4,128]{3,0,2,1:T(8,128)(2,1)} %bitcast.140, bf16[4096,2,128,1]{2,1,0,3:T(2,128)(2,1)} %bitcast.123), kind=kOutput, calls=%fused_computation.118 | convolution fusion | flops 1098911744 | bytes 11276288 | tf_op jit(solution)/shard_map/sub | solution.py:190
  252.9 4.7 fusion.79
  257.6 1.7 all-gather.5.cloned.1.call-done
  259.2 9.8 %convolution_convert_fusion.3 = bf16[128,8192]{1,0:T(8,128)(2,1)} fusion(bf16[128,1024]{0,1:T(8,128)(2,1)S(1)} %bitcast.127, bf16[1024,8192]{1,0:T(8,128)(2,1)} %all-gather.5.cloned.1.call-done), kind=kOutput, calls=%fused_computation.24 | convolution fusion | flops 2148532224 | bytes 19136512 | tf_op jit(solution)/shard_map/dot_general | solution.py:250
  269.0 11.1 %fusion.128 = (f32[2,4,128]{2,1,0:T(4,128)S(1)}, bf16[2,4,128,4096]{2,3,1,0:T(8,128)(2,1)}) fusion(pred[128,4096]{0,1:T(8,128)(4,1)S(1)} %get-tuple-element.35, bf16[128,2,4,128]{3,0,2,1:T(8,128)(2,1)} %bitcast.139, bf16[4096,2,128,1]{2,1,0,3:T(2,128)(2,1)S(1)} %bitcast.124), kind=kOutput, calls=%fused_computation.119 | convolution fusion | flops 1098911744 | bytes 11276288 | tf_op jit(solution)/shard_map/sub | solution.py:190
  280.1 5.3 fusion.76
  285.4 9.6 %convolution_convert_fusion.2 = bf16[128,8192]{1,0:T(8,128)(2,1)} fusion(bf16[128,1024]{0,1:T(8,128)(2,1)S(1)} %bitcast.129, bf16[1024,8192]{1,0:T(8,128)(2,1)} %all-gather.5.cloned.1.call-done), kind=kOutput, calls=%fused_computation.23 | convolution fusion | flops 2148532224 | bytes 19136512 | tf_op jit(solution)/shard_map/dot_general | solution.py:250
  295.0 11.4 %fusion.133 = (f32[2,4,128]{2,1,0:T(4,128)S(1)}, bf16[2,4,128,4096]{2,3,1,0:T(8,128)(2,1)}) fusion(pred[128,4096]{0,1:T(8,128)(4,1)} %get-tuple-element.36, bf16[128,2,4,128]{3,0,2,1:T(8,128)(2,1)S(1)} %bitcast.138, bf16[4096,2,128,1]{2,1,0,3:T(2,128)(2,1)S(1)} %bitcast.125), kind=kOutput, calls=%fused_computation.120 | convolution fusion | flops 1098911744 | bytes 11276288 | tf_op jit(solution)/shard_map/sub | solution.py:190
  306.4 5.3 fusion.73
  311.7 9.6 %convolution_convert_fusion.1 = bf16[128,8192]{1,0:T(8,128)(2,1)} fusion(bf16[128,1024]{0,1:T(8,128)(2,1)S(1)} %bitcast.131, bf16[1024,8192]{1,0:T(8,128)(2,1)} %all-gather.5.cloned.1.call-done), kind=kOutput, calls=%fused_computation.22 | convolution fusion | flops 2148532224 | bytes 19136512 | tf_op jit(solution)/shard_map/dot_general | solution.py:250
  321.3 10.9 %fusion.138 = (f32[2,4,128]{2,1,0:T(4,128)S(1)}, bf16[2,4,128,4096]{2,3,1,0:T(8,128)(2,1)}) fusion(pred[128,4096]{0,1:T(8,128)(4,1)S(1)} %get-tuple-element.37, bf16[128,2,4,128]{3,0,2,1:T(8,128)(2,1)} %bitcast.137, bf16[4096,2,128,1]{2,1,0,3:T(2,128)(2,1)S(1)} %bitcast.126), kind=kOutput, calls=%fused_computation.121 | convolution fusion | flops 1098911744 | bytes 11276288 | tf_op jit(solution)/shard_map/sub | solution.py:190
  332.2 5.3 fusion.70
  337.5 9.6 %convolution_convert_fusion = bf16[128,8192]{1,0:T(8,128)(2,1)} fusion(bf16[128,1024]{0,1:T(8,128)(2,1)S(1)} %bitcast.133, bf16[1024,8192]{1,0:T(8,128)(2,1)} %all-gather.5.cloned.1.call-done), kind=kOutput, calls=%fused_computation.21 | convolution fusion | flops 2148532224 | bytes 19136512 | tf_op jit(solution)/shard_map/dot_general | solution.py:250
  347.0 0.0 reduce-scatter.11.cloned.1.call-update
  347.1 0.0 reduce-scatter.9.cloned.1.call-start
  347.1 0.5 reduce-scatter.9.cloned.1.call-update
  347.7 0.0 reduce-scatter.7.cloned.1.call-start
  347.7 0.5 reduce-scatter.7.cloned.1.call-update
  348.2 0.0 reduce-scatter.5.cloned.1.call-start
  348.3 0.5 reduce-scatter.5.cloned.1.call-update
  348.8 0.1 copy.28
  349.0 0.1 copy.31
  349.1 0.1 copy.30
  349.3 0.1 copy.29
  349.4 1.0 pad_maximum_fusion.1
  350.5 40.4 %reduce-scatter.11.cloned.1.call-done = bf16[128,2048]{1,0:T(8,128)(2,1)} async-done(((bf16[128,8192]{1,0:T(8,128)(2,1)}), bf16[128,2048]{1,0:T(8,128)(2,1)}) %reduce-scatter.11.cloned.1.call-update) | async-done | bytes 524304 | tf_op jit(solution)/shard_map/reduce_scatter | solution.py:205
  390.9 45.0 %reduce-scatter.9.cloned.1.call-done = bf16[128,2048]{1,0:T(8,128)(2,1)} async-done(((bf16[128,8192]{1,0:T(8,128)(2,1)}), bf16[128,2048]{1,0:T(8,128)(2,1)}) %reduce-scatter.9.cloned.1.call-update) | async-done | bytes 524304 | tf_op jit(solution)/shard_map/reduce_scatter | solution.py:205
  435.9 45.0 %reduce-scatter.7.cloned.1.call-done = bf16[128,2048]{1,0:T(8,128)(2,1)} async-done(((bf16[128,8192]{1,0:T(8,128)(2,1)}), bf16[128,2048]{1,0:T(8,128)(2,1)}) %reduce-scatter.7.cloned.1.call-update) | async-done | bytes 524304 | tf_op jit(solution)/shard_map/reduce_scatter | solution.py:205
  480.9 45.0 %reduce-scatter.5.cloned.1.call-done = bf16[128,2048]{1,0:T(8,128)(2,1)} async-done(((bf16[128,8192]{1,0:T(8,128)(2,1)}), bf16[128,2048]{1,0:T(8,128)(2,1)}) %reduce-scatter.5.cloned.1.call-update) | async-done | bytes 524304 | tf_op jit(solution)/shard_map/reduce_scatter | solution.py:205
  525.9 3.8 add_convert_fusion
  (27 shorter events, 0.2 us)
Async XLA Ops:
  7.2 146.4 %all-gather.3.cloned.1.call-start = ((), (), s32[]{:S(2)}) async-start(), calls=%async_computation.4 | async-start | bytes 28311552 | tf_op jit(solution)/shard_map/all_gather | solution.py:212
  10.5 143.2 %copy-start.6 = (s32[512]{0:T(512)S(1)}, s32[512]{0:T(512)}, u32[]{:S(2)}) copy-start(s32[512]{0:T(512)} %param.11) | copy-start | bytes 6148
  10.5 143.2 %copy-start.7 = (f32[1024]{0:T(1024)S(1)}, f32[1024]{0:T(1024)}, u32[]{:S(2)}) copy-start(f32[1024]{0:T(1024)} %param.16) | copy-start | bytes 12292
  10.5 143.2 %copy-start.8 = (f32[256]{0:T(256)S(1)}, f32[256]{0:T(256)}, u32[]{:S(2)}) copy-start(f32[256]{0:T(256)} %param.18) | copy-start | bytes 3076
  10.5 143.2 %copy-start.9 = (f32[256]{0:T(256)S(1)}, f32[256]{0:T(256)}, u32[]{:S(2)}) copy-start(f32[256]{0:T(256)} %param.17) | copy-start | bytes 3076
  10.5 248.7 %all-gather.5.cloned.1.call-start = ((), (), s32[]{:S(2)}) async-start(), calls=%async_computation.5 | async-start | bytes 18874368 | tf_op jit(solution)/shard_map/all_gather | solution.py:218
  10.6 149.4 %copy-start.10 = (f32[8192]{0:T(1024)S(1)}, f32[8192]{0:T(1024)}, u32[]{:S(2)}) copy-start(f32[8192]{0:T(1024)} %param.12) | copy-start | bytes 98308
  153.6 237.3 %reduce-scatter.11.cloned.1.call-start = ((), (), s32[]{:S(2)}) async-start(), calls=%async_computation.9 | async-start | bytes 2621440 | tf_op jit(solution)/shard_map/reduce_scatter | solution.py:205
  154.8 5.9 %copy-start = (bf16[512,8192]{1,0:T(8,128)(2,1)S(1)}, bf16[512,8192]{1,0:T(8,128)(2,1)}, u32[]{:S(2)}) copy-start(bf16[512,8192]{1,0:T(8,128)(2,1)} %shard_map.113) | copy-start | bytes 25165828
  179.4 1.7 copy-start.1
  240.1 12.8 %copy-start.4 = (bf16[4096,2,128,1]{0,2,3,1:T(8,128)(2,1)S(1)}, bf16[4096,2,128,1]{0,2,3,1:T(8,128)(2,1)}, u32[]{:S(2)}) copy-start(bf16[4096,2,128,1]{0,2,3,1:T(8,128)(2,1)} %copy.34) | copy-start | bytes 6291460
  259.2 9.8 %copy-start.3 = (bf16[4096,2,128]{2,1,0:T(2,128)(2,1)S(1)}, bf16[4096,2,128]{2,1,0:T(2,128)(2,1)}, u32[]{:S(2)}) copy-start(bf16[4096,2,128]{2,1,0:T(2,128)(2,1)} %reshape.221) | copy-start | bytes 6291460
  285.4 9.6 %copy-start.5 = (bf16[128,8,128]{2,0,1:T(8,128)(2,1)S(1)}, bf16[128,8,128]{2,0,1:T(8,128)(2,1)}, u32[]{:S(2)}) copy-start(bf16[128,8,128]{2,0,1:T(8,128)(2,1)} %copy.17) | copy-start | bytes 786436
  347.1 88.8 %reduce-scatter.9.cloned.1.call-start = ((), (), s32[]{:S(2)}) async-start(), calls=%async_computation.8 | async-start | bytes 2621440 | tf_op jit(solution)/shard_map/reduce_scatter | solution.py:205
  347.6 178.3 %copy-start.2 = (bf16[512,2048]{1,0:T(8,128)(2,1)S(1)}, bf16[512,2048]{1,0:T(8,128)(2,1)}, u32[]{:S(2)}) copy-start(bf16[512,2048]{1,0:T(8,128)(2,1)} %src.1) | copy-start | bytes 6291460
  347.7 133.2 %reduce-scatter.7.cloned.1.call-start = ((), (), s32[]{:S(2)}) async-start(), calls=%async_computation.7 | async-start | bytes 2621440 | tf_op jit(solution)/shard_map/reduce_scatter | solution.py:205
  348.2 177.7 %reduce-scatter.5.cloned.1.call-start = ((), (), s32[]{:S(2)}) async-start(), calls=%async_computation.6 | async-start | bytes 2621440 | tf_op jit(solution)/shard_map/reduce_scatter | solution.py:205
Sparse Core Ops, SparseCore 0:
  10.6 127.9 all-gather.2
  153.7 105.4 all-gather.4
  347.2 43.6 reduce-scatter.10
  393.1 42.8 reduce-scatter.8
  438.1 42.8 reduce-scatter.6
  483.1 42.8 reduce-scatter.4
